TPU v7x, 32 devices: a whole 2x2x4 slice. The times are simulated.
32 devices in a mesh: lat: 8 (over z, y), rad: 4 (over x, core).
Axes of the slice: x: 2, y: 2, z: 4, core: 2. Of those that a mesh axis runs over, the one named last changes fastest.
Arguments:
- displacement: float32 [64, 6144], P('rad', 'lat'), may hold values from -6 to 6
- surface_load: float32 [64, 6144], P('rad', 'lat'), may hold values from -6 to 6
- dens_grad: float32 [64, 6144], P('rad', 'lat'), may hold values from 0.5 to 2
- dens_ref: float32 [64], P('rad'), may hold values from 0.5 to 2
- relax_rate: float32 [64, 6144], P('rad', 'lat'), may hold values from 0.02 to 0.2
- basis: bfloat16 [2408, 6144], P(None, 'lat'), may hold values from -0.109375 to 0.109375
- neighbours: int32 [4, 6144], P(None, 'lat'), may hold values from 0 to 767
- green: float32 [49, 64, 64], replicated, may hold values from -2.5 to 2.5
Outputs:
- relaxed: float32 [64, 6144], P('rad', 'lat')
- step_sizes: float32 [3], replicated
Inputs may be any that keep to these rules, and one draw needn't show every extreme that they name: `neighbours`: indices of columns inside the same tile of 768 columns.
All inputs are finite; a program needn't handle non-finite values.
Results may differ from a plain program's by a relative error of at most 0.0045.
Values may be sent and summed in bfloat16 or wider, within the bound.
No kernel may reach another device: no remote copies, remote signals or barrier semaphores. Data moves between devices by JAX's collectives and lax.ppermute only.
A program may use at most 64 MiB of HBM per device.

v0:
```python
import jax
import jax.numpy as jnp
from jax import lax
from jax.sharding import PartitionSpec as P

DEG = 48
L = 64
ITERS = 3
KH = 2401


def extended(shard, sides, width):
    for axis, dim in sides:
        size, length = (lax.axis_size(axis), shard.shape[dim])
        up = [(i, (i + 1) % size) for i in range(size - 1)]
        down = [(j, i) for i, j in up]
        last = lax.slice_in_dim(shard, length - width, length, axis=dim)
        first = lax.slice_in_dim(shard, 0, width, axis=dim)
        before = lax.ppermute(last, axis, up)
        after = lax.ppermute(first, axis, down)
        shard = jnp.concatenate([before, shard, after], axis=dim)
    return shard


def apply_degrees(coefs, green_rows):
    blocks = []
    for degree in range(DEG + 1):
        rows = coefs[degree * degree : (degree + 1) * (degree + 1)]
        blocks.append(
            lax.dot_general(
                rows,
                green_rows[degree],
                (((1,), (1,)), ((), ())),
                precision=lax.Precision.HIGHEST,
                preferred_element_type=jnp.float32,
            )
        )
    blocks.append(jnp.zeros((coefs.shape[0] - KH, green_rows.shape[1]), jnp.float32))
    return jnp.concatenate(blocks, axis=0).astype(jnp.bfloat16)


def local(displacement, surface_load, dens_grad, dens_ref, relax_rate, basis, neighbours, green):
    u = displacement
    layers, columns = u.shape
    lat_count = lax.axis_size("lat")
    green_rows = lax.dynamic_slice_in_dim(green, lax.axis_index("rad") * layers, layers, 1)
    sizes = []
    for it in range(ITERS):
        padded = extended(u, (("rad", 0),), 1)
        rho = (dens_grad * u + dens_ref[:, None] * (padded[2:] - padded[:-2]) * 0.5).astype(
            jnp.bfloat16
        )
        partial_sums = lax.dot_general(
            basis, rho, (((1,), (1,)), ((), ())), preferred_element_type=jnp.float32
        )
        summed = lax.psum(partial_sums, "lat")
        coefs = lax.all_gather(summed, "rad", axis=1, tiled=True)
        phi = apply_degrees(coefs, green_rows)
        potential = lax.dot_general(
            phi, basis, (((0,), (0,)), ((), ())), preferred_element_type=jnp.float32
        )
        outer = extended(potential, (("rad", 0),), 1)
        force = (outer[2:] - outer[:-2]) * 0.5
        lap = jnp.sum(u[:, neighbours], axis=1) - 4.0 * u
        new = u + relax_rate * (surface_load + force + lap - u)
        squared = jnp.sum((new - u) ** 2)
        sizes.append(squared)
        u = new
    totals = jnp.stack(sizes)
    totals = lax.psum(totals, ("lat", "rad"))
    return (u, jnp.sqrt(totals / (L * columns * lat_count)))


def solution(mesh):
    placed = (
        P("rad", "lat"),
        P("rad", "lat"),
        P("rad", "lat"),
        P("rad"),
        P("rad", "lat"),
        P(None, "lat"),
        P(None, "lat"),
        P(),
    )
    return jax.shard_map(
        local, mesh=mesh, in_specs=placed, out_specs=(P("rad", "lat"), P()), check_vma=False
    )
```

profile of v0, /device:TPU:0, one launch (start us, length us, event | category | flops | bytes accessed | tf_op | source)
XLA Modules:
  0.0 424.7 jit_solution(13441633414190941219)
XLA Ops:
  7.2 0.9 fusion.406
  8.1 2.4 collective-permute-start.1
  10.5 1.3 collective-permute-start
  11.8 3.8 collective-permute-done
  15.6 3.9 convolution_bitcast_fusion.2
  19.7 72.3 %all-reduce.4.cloned.1.call-done = f32[2408,16]{0,1:T(8,128)} async-done(((f32[2408,16]{0,1:T(8,128)}), f32[2408,16]{0,1:T(8,128)}) %all-reduce.4.cloned.1.call-update) | async-done | bytes 154128 | tf_op jit(solution)/shard_map/psum | solution.py:56
  92.0 7.9 %all_gather.9 = f32[2408,64]{0,1:T(8,128)S(1)} all-gather(f32[2408,16]{0,1:T(8,128)} %all-reduce.4.cloned.1.call-done), channel_id=1, replica_groups=mesh['lat'=8,'rad'=4] {'rad'}, dimensions={1}, use_global_device_ids=true | all-gather | bytes 770560 | tf_op jit(solution)/shard_map/all_gather | solution.py:57
  101.4 0.3 convolution_convert_fusion.134
  112.0 2.7 fusion.407
  114.7 2.3 collective-permute-start.3
  116.9 1.3 collective-permute-start.2
  118.4 10.8 %gather_fusion = f32[3072,16]{1,0:T(8,128)} fusion(f32[16,768]{0,1:T(8,128)S(1)} %copy.24, s32[3072]{0:T(1024)S(1)} %broadcast_clamp_fusion), kind=kCustom, calls=%fused_computation | custom fusion | bytes 405504 | tf_op jit(solution)/shard_map/gather | solution.py:64
  129.3 1.6 reduce.3
  131.1 3.0 collective-permute-start.5
  134.1 1.3 collective-permute-start.4
  135.5 2.8 collective-permute-done.4
  138.3 3.8 convolution_bitcast_fusion.1
  142.1 70.9 %all-reduce.6.cloned.1.call-done = f32[2408,16]{0,1:T(8,128)} async-done(((f32[2408,16]{0,1:T(8,128)}), f32[2408,16]{0,1:T(8,128)}) %all-reduce.6.cloned.1.call-update) | async-done | bytes 154128 | tf_op jit(solution)/shard_map/psum | solution.py:56
  213.1 7.9 %all_gather.10 = f32[2408,64]{0,1:T(8,128)S(1)} all-gather(f32[2408,16]{0,1:T(8,128)} %all-reduce.6.cloned.1.call-done), channel_id=1, replica_groups=mesh['lat'=8,'rad'=4] {'rad'}, dimensions={1}, use_global_device_ids=true | all-gather | bytes 770560 | tf_op jit(solution)/shard_map/all_gather | solution.py:57
  221.3 0.3 convolution_convert_fusion.138
  221.9 0.3 convolution_convert_fusion.89
  222.2 0.3 convolution_convert_fusion.88
  222.5 0.3 convolution_convert_fusion.87
  222.8 0.3 convolution_convert_fusion.86
  233.1 2.6 fusion.408
  235.7 2.3 collective-permute-start.7
  238.0 1.3 collective-permute-start.6
  239.4 10.8 %gather_fusion.1 = f32[3072,16]{1,0:T(8,128)} fusion(f32[16,768]{0,1:T(8,128)S(1)} %copy.34, s32[3072]{0:T(1024)S(1)} %broadcast_clamp_fusion), kind=kCustom, calls=%fused_computation.1 | custom fusion | bytes 405504 | tf_op jit(solution)/shard_map/gather | solution.py:64
  250.3 1.6 reduce.4
  252.0 3.0 collective-permute-start.9
  255.1 1.3 collective-permute-start.8
  256.4 2.8 collective-permute-done.8
  259.2 3.8 convolution_bitcast_fusion
  263.0 71.0 %all-reduce.8.cloned.1.call-done = f32[2408,16]{0,1:T(8,128)} async-done(((f32[2408,16]{0,1:T(8,128)}), f32[2408,16]{0,1:T(8,128)}) %all-reduce.8.cloned.1.call-update) | async-done | bytes 154128 | tf_op jit(solution)/shard_map/psum | solution.py:56
  334.0 8.1 %all_gather.11 = f32[2408,64]{0,1:T(8,128)S(1)} all-gather(f32[2408,16]{0,1:T(8,128)} %all-reduce.8.cloned.1.call-done), channel_id=1, replica_groups=mesh['lat'=8,'rad'=4] {'rad'}, dimensions={1}, use_global_device_ids=true | all-gather | bytes 770560 | tf_op jit(solution)/shard_map/all_gather | solution.py:57
  343.0 0.3 convolution_convert_fusion.44
  343.3 0.3 convolution_convert_fusion.43
  343.6 0.3 convolution_convert_fusion.42
  343.9 0.3 convolution_convert_fusion.41
  354.2 2.6 fusion.409
  356.8 2.3 collective-permute-start.11
  359.1 1.3 collective-permute-start.10
  360.6 10.8 %gather_fusion.2 = f32[3072,16]{1,0:T(8,128)} fusion(f32[16,768]{0,1:T(8,128)S(1)} %copy.44, s32[3072]{0:T(1024)S(1)} %broadcast_clamp_fusion), kind=kCustom, calls=%fused_computation.2 | custom fusion | bytes 405504 | tf_op jit(solution)/shard_map/gather | solution.py:64
  371.4 1.6 reduce.5
  373.1 1.4 multiply_reduce_fusion.2
  374.4 2.0 pad_maximum_fusion.12
  376.4 41.3 %psum.31 = f32[3]{0:T(128)S(1)} all-reduce(f32[3]{0:T(128)S(1)} %pad_maximum_fusion.12), channel_id=1, replica_groups=mesh['lat'=8,'rad'=4] {'lat','rad'}, use_global_device_ids=true, to_apply=%region_9.0 | all-reduce | flops 3 | bytes 24 | tf_op jit(solution)/shard_map/psum | solution.py:70
  417.7 0.5 multiply_sqrt_fusion
  (213 shorter events, 34.4 us)
Async XLA Ops:
  7.2 92.8 %copy-start = (f32[49,64,64]{2,1,0:T(8,128)S(1)}, f32[49,64,64]{2,1,0:T(8,128)}, u32[]{:S(2)}) copy-start(f32[49,64,64]{2,1,0:T(8,128)} %param.15) | copy-start | bytes 2408452
  7.2 84.8 %all-reduce.4.cloned.1.call-start = ((), (), s32[]{:S(2)}) async-start(), calls=%async_computation | async-start | bytes 311296 | tf_op jit(solution)/shard_map/psum | solution.py:56
  8.1 3.7 collective-permute-start.1
  10.5 5.2 %collective-permute-start = (f32[1,768]{1,0:T(1,128)S(1)}, f32[1,768]{1,0:T(1,128)S(1)}, u32[]{:S(2)}, u32[]{:S(2)}) collective-permute-start(f32[1,768]{1,0:T(1,128)S(1)} %get-tuple-element.16), channel_id=1, source_target_pairs={{1,0},{2,1},{3,2},{5,4},{6,5},{7,6},{9,8},{10,9},{11,10},{13,12},{... | collective-permute-start | bytes 9224 | tf_op jit(solution)/shard_map/ppermute | solution.py:20
  11.8 7.8 %copy-start.5 = (s32[4,768]{1,0:T(4,128)S(1)}, s32[4,768]{1,0:T(4,128)}, u32[]{:S(2)}) copy-start(s32[4,768]{1,0:T(4,128)} %param.14) | copy-start | bytes 36868
  19.6 193.5 %all-reduce.6.cloned.1.call-start = ((), (), s32[]{:S(2)}) async-start(), calls=%async_computation.1 | async-start | bytes 311296 | tf_op jit(solution)/shard_map/psum | solution.py:56
  112.0 6.3 %copy-start.1 = (f32[16,768]{1,0:T(8,128)S(1)}, f32[16,768]{1,0:T(8,128)}, u32[]{:S(2)}) copy-start(f32[16,768]{1,0:T(8,128)} %param.8) | copy-start | bytes 147460
  114.7 16.3 %collective-permute-start.3 = (f32[1,768]{1,0:T(1,128)S(1)}, f32[1,768]{1,0:T(1,128)S(1)}, u32[]{:S(2)}, u32[]{:S(2)}) collective-permute-start(f32[1,768]{1,0:T(1,128)S(1)} %get-tuple-element.15), channel_id=1, source_target_pairs={{0,1},{1,2},{2,3},{4,5},{5,6},{6,7},{8,9},{9,10},{10,11},{12,13},{... | collective-permute-start | bytes 9224 | tf_op jit(solution)/shard_map/ppermute | solution.py:19
  116.9 14.1 %collective-permute-start.2 = (f32[1,768]{1,0:T(1,128)S(1)}, f32[1,768]{1,0:T(1,128)S(1)}, u32[]{:S(2)}, u32[]{:S(2)}) collective-permute-start(f32[1,768]{1,0:T(1,128)S(1)} %get-tuple-element.14), channel_id=1, source_target_pairs={{1,0},{2,1},{3,2},{5,4},{6,5},{7,6},{9,8},{10,9},{11,10},{13,12},{... | collective-permute-start | bytes 9224 | tf_op jit(solution)/shard_map/ppermute | solution.py:20
  129.3 1.8 copy-start.3
  129.3 1.8 copy-start.4
  129.3 9.0 %copy-start.2 = (f32[16,768]{1,0:T(8,128)S(1)}, f32[16,768]{1,0:T(8,128)}, u32[]{:S(2)}) copy-start(f32[16,768]{1,0:T(8,128)} %param.10) | copy-start | bytes 147460
  129.3 9.0 %copy-start.6 = (f32[16]{0:T(128)S(1)}, f32[16]{0:T(128)}, u32[]{:S(2)}) copy-start(f32[16]{0:T(128)} %param.11) | copy-start | bytes 196
  131.1 4.3 %collective-permute-start.5 = (f32[1,768]{1,0:T(1,128)S(1)}, f32[1,768]{1,0:T(1,128)S(1)}, u32[]{:S(2)}, u32[]{:S(2)}) collective-permute-start(f32[1,768]{1,0:T(1,128)S(1)} %get-tuple-element.13), channel_id=1, source_target_pairs={{0,1},{1,2},{2,3},{4,5},{5,6},{6,7},{8,9},{9,10},{10,11},{12,13},{... | collective-permute-start | bytes 9224 | tf_op jit(solution)/shard_map/ppermute | solution.py:19
  134.1 4.1 collective-permute-start.4
  142.1 191.9 %all-reduce.8.cloned.1.call-start = ((), (), s32[]{:S(2)}) async-start(), calls=%async_computation.2 | async-start | bytes 311296 | tf_op jit(solution)/shard_map/psum | solution.py:56
  235.7 16.2 %collective-permute-start.7 = (f32[1,768]{1,0:T(1,128)S(1)}, f32[1,768]{1,0:T(1,128)S(1)}, u32[]{:S(2)}, u32[]{:S(2)}) collective-permute-start(f32[1,768]{1,0:T(1,128)S(1)} %get-tuple-element.11), channel_id=1, source_target_pairs={{0,1},{1,2},{2,3},{4,5},{5,6},{6,7},{8,9},{9,10},{10,11},{12,13},{... | collective-permute-start | bytes 9224 | tf_op jit(solution)/shard_map/ppermute | solution.py:19
  238.0 14.0 %collective-permute-start.6 = (f32[1,768]{1,0:T(1,128)S(1)}, f32[1,768]{1,0:T(1,128)S(1)}, u32[]{:S(2)}, u32[]{:S(2)}) collective-permute-start(f32[1,768]{1,0:T(1,128)S(1)} %get-tuple-element.10), channel_id=1, source_target_pairs={{1,0},{2,1},{3,2},{5,4},{6,5},{7,6},{9,8},{10,9},{11,10},{13,12},{... | collective-permute-start | bytes 9224 | tf_op jit(solution)/shard_map/ppermute | solution.py:20
  252.0 4.3 %collective-permute-start.9 = (f32[1,768]{1,0:T(1,128)S(1)}, f32[1,768]{1,0:T(1,128)S(1)}, u32[]{:S(2)}, u32[]{:S(2)}) collective-permute-start(f32[1,768]{1,0:T(1,128)S(1)} %get-tuple-element.9), channel_id=1, source_target_pairs={{0,1},{1,2},{2,3},{4,5},{5,6},{6,7},{8,9},{9,10},{10,11},{12,13},{... | collective-permute-start | bytes 9224 | tf_op jit(solution)/shard_map/ppermute | solution.py:19
  255.1 4.1 collective-permute-start.8
  356.8 16.2 %collective-permute-start.11 = (f32[1,768]{1,0:T(1,128)S(1)}, f32[1,768]{1,0:T(1,128)S(1)}, u32[]{:S(2)}, u32[]{:S(2)}) collective-permute-start(f32[1,768]{1,0:T(1,128)S(1)} %get-tuple-element.7), channel_id=1, source_target_pairs={{0,1},{1,2},{2,3},{4,5},{5,6},{6,7},{8,9},{9,10},{10,11},{12,13},{... | collective-permute-start | bytes 9224 | tf_op jit(solution)/shard_map/ppermute | solution.py:19
  359.1 14.0 %collective-permute-start.10 = (f32[1,768]{1,0:T(1,128)S(1)}, f32[1,768]{1,0:T(1,128)S(1)}, u32[]{:S(2)}, u32[]{:S(2)}) collective-permute-start(f32[1,768]{1,0:T(1,128)S(1)} %get-tuple-element.6), channel_id=1, source_target_pairs={{1,0},{2,1},{3,2},{5,4},{6,5},{7,6},{9,8},{10,9},{11,10},{13,12},{... | collective-permute-start | bytes 9224 | tf_op jit(solution)/shard_map/ppermute | solution.py:20
Sparse Core Ops, SparseCore 0:
  19.7 72.2 all-reduce.3
  142.2 70.8 all-reduce.5
  263.1 70.8 all-reduce.7
where the time goes:
time: 426 us; the launch traced here: 425 us
  waiting for transfers between devices  224 us (53%)
  blocking collectives  65.1 us (15%)
  matrix products  52.3 us (12%)
  local copies, waits for them, and re-layouts  37.5 us (9%)
  starting transfers between devices  23.1 us (5%)
  between operations  14.2 us (3%)
  other arithmetic  8.64 us (2%)
    psum x3, waiting for transfers between devices, local(): summed = lax.psum(partial_sums, 'lat')  214 us
    psum x1, blocking collectives, local(): totals = lax.psum(totals, ('lat', 'rad'))  41.3 us
    dot_general x147, matrix products, apply_degrees(): lax.dot_general(rows, green_rows[degree], (((1,), (1,)), ((), ())), preci...  32.9 us
    gather x3, local copies, waits for them, and re-layouts, local(): lap = jnp.sum(u[:, neighbours], axis=1) - 4.0 * u  32.5 us
    all_gather x3, blocking collectives, local(): coefs = lax.all_gather(summed, 'rad', axis=1, tiled=True)  23.9 us
    ppermute x6, starting transfers between devices, extended(): before = lax.ppermute(last, axis, up)  15.2 us
    dot_general x3, matrix products, local(): lax.dot_general(basis, rho, (((1,), (1,)), ((), ())), preferred_element_t...  11.5 us
    ppermute x6, waiting for transfers between devices, extended(): after = lax.ppermute(first, axis, down)  9.47 us
  transfers between devices with their start and end apart: 15, of which 6 were waited for; matrix products, arithmetic and copies ran while one was open for 9% of the time, Pallas kernels for 0%

commit v1 on v0

--- a/solution.py
+++ b/solution.py
@@ -53,7 +53,9 @@
         partial_sums = lax.dot_general(
             basis, rho, (((1,), (1,)), ((), ())), preferred_element_type=jnp.float32
         )
-        summed = lax.psum(partial_sums, "lat")
+        summed = partial_sums
+        for hop in (1, 2, 4):
+            summed = summed + lax.ppermute(summed, "lat", [(dev, dev ^ hop) for dev in range(8)])
         coefs = lax.all_gather(summed, "rad", axis=1, tiled=True)
         phi = apply_degrees(coefs, green_rows)
         potential = lax.dot_general(

time: 426 us -> 262 us (0.62)
  waiting for transfers between devices: 224 us -> 64.8 us
  starting transfers between devices: 23.1 us -> 37.3 us
  between operations: 14.2 us -> 1.1 us
    psum x3 -> x0, waiting for transfers between devices: 214 us -> none  [local(): summed = lax.psum(partial_sums, 'lat')]
    ppermute x0 -> x9, waiting for transfers between devices: none -> 55 us  [local(): lax.ppermute(summed, 'lat', [(dev, dev ^ hop) for dev in range(8)])]
    ppermute x0 -> x9, starting transfers between devices: none -> 12.8 us  [local(): lax.ppermute(summed, 'lat', [(dev, dev ^ hop) for dev in range(8)])]
  transfers between devices with their start and end apart: 15 -> 21, of which waited for: 6 -> 12; matrix products, arithmetic and copies ran while one was open for 9% -> 15% of each run, Pallas kernels for 0% -> 0%
where the time goes in v1:
time: 262 us; the launch traced here: 261 us
  waiting for transfers between devices  64.8 us (25%)
  blocking collectives  61 us (23%)
  matrix products  50.3 us (19%)
  local copies, waits for them, and re-layouts  37.6 us (14%)
  starting transfers between devices  37.3 us (14%)
  other arithmetic  8.83 us (3%)
    ppermute x9, waiting for transfers between devices, local(): lax.ppermute(summed, 'lat', [(dev, dev ^ hop) for dev in range(8)])  55 us
    psum x1, blocking collectives, local(): totals = lax.psum(totals, ('lat', 'rad'))  40 us
    dot_general x147, matrix products, apply_degrees(): lax.dot_general(rows, green_rows[degree], (((1,), (1,)), ((), ())), preci...  32.9 us
    gather x3, local copies, waits for them, and re-layouts, local(): lap = jnp.sum(u[:, neighbours], axis=1) - 4.0 * u  32.5 us
    all_gather x3, blocking collectives, local(): coefs = lax.all_gather(summed, 'rad', axis=1, tiled=True)  21 us
    ppermute x6, starting transfers between devices, extended(): before = lax.ppermute(last, axis, up)  16.7 us
    ppermute x9, starting transfers between devices, local(): lax.ppermute(summed, 'lat', [(dev, dev ^ hop) for dev in range(8)])  12.8 us
    ppermute x6, waiting for transfers between devices, extended(): after = lax.ppermute(first, axis, down)  9.83 us
  transfers between devices with their start and end apart: 21, of which 12 were waited for; matrix products, arithmetic and copies ran while one was open for 15% of the time, Pallas kernels for 0%

profile of v1, /device:TPU:0, one launch (start us, length us, event | category | flops | bytes accessed | tf_op | source)
XLA Modules:
  0.0 260.9 jit_solution(5909004982219384565)
XLA Ops:
  1.5 2.4 collective-permute-start.1
  3.9 1.3 collective-permute-start
  5.2 3.8 %collective-permute-done = f32[1,768]{1,0:T(1,128)S(1)} collective-permute-done((f32[1,768]{1,0:T(1,128)S(1)}, f32[1,768]{1,0:T(1,128)S(1)}, u32[]{:S(2)}, u32[]{:S(2)}) %collective-permute-start) | collective-permute-done | bytes 3104 | tf_op jit(solution)/shard_map/ppermute | solution.py:20
  9.1 3.2 %convolution_bitcast_fusion.2 = f32[2408,16]{0,1:T(8,128)S(1)} fusion(bf16[2408,768]{1,0:T(8,128)(2,1)} %param.13, f32[16,768]{1,0:T(8,128)} %param.8, f32[1,768]{1,0:T(1,128)S(1)} %collective-permute-done.1, f32[1,768]{1,0:T(1,128)S(1)} %collective-permute-done, f32[16,768]{1,0:T(8,128)} %param.10, f32[16]{0:T(128)} %param.11), kind=kOutput, calls=%fused_computation.5 | convolution fusion | flops 59277312 | bytes 3957312 | tf_op jit(solution)/shard_map/dot_general | solution.py:53
  12.3 1.5 collective-permute-start.2
  13.9 4.0 %collective-permute-done.2 = f32[2408,16]{0,1:T(8,128)S(1)} collective-permute-done((f32[2408,16]{0,1:T(8,128)S(1)}, f32[2408,16]{0,1:T(8,128)S(1)}, u32[]{:S(2)}, u32[]{:S(2)}) %collective-permute-start.2) | collective-permute-done | bytes 154144 | tf_op jit(solution)/shard_map/ppermute | solution.py:58
  17.9 1.6 collective-permute-start.3
  19.5 5.1 %collective-permute-done.3 = f32[2408,16]{0,1:T(8,128)S(1)} collective-permute-done((f32[2408,16]{0,1:T(8,128)S(1)}, f32[2408,16]{0,1:T(8,128)S(1)}, u32[]{:S(2)}, u32[]{:S(2)}) %collective-permute-start.3) | collective-permute-done | bytes 154144 | tf_op jit(solution)/shard_map/ppermute | solution.py:58
  24.6 2.7 %collective-permute-start.4 = (f32[2408,16]{0,1:T(8,128)S(1)}, f32[2408,16]{0,1:T(8,128)S(1)}, u32[]{:S(2)}, u32[]{:S(2)}) collective-permute-start(f32[2408,16]{0,1:T(8,128)S(1)} %add.75), channel_id=1, source_target_pairs={{0,16},{4,20},{8,24},{12,28},{16,0},{20,4},{24,8},{28,12},{1,17},{... | collective-permute-start | bytes 462344 | tf_op jit(solution)/shard_map/ppermute | solution.py:58
  27.3 7.7 %collective-permute-done.4 = f32[2408,16]{0,1:T(8,128)S(1)} collective-permute-done((f32[2408,16]{0,1:T(8,128)S(1)}, f32[2408,16]{0,1:T(8,128)S(1)}, u32[]{:S(2)}, u32[]{:S(2)}) %collective-permute-start.4) | collective-permute-done | bytes 154144 | tf_op jit(solution)/shard_map/ppermute | solution.py:58
  35.0 6.8 %all_gather.9 = f32[2408,64]{0,1:T(8,128)S(1)} all-gather(f32[2408,16]{0,1:T(8,128)S(1)} %add.76), channel_id=1, replica_groups=mesh['lat'=8,'rad'=4] {'rad'}, dimensions={1}, use_global_device_ids=true | all-gather | bytes 770560 | tf_op jit(solution)/shard_map/all_gather | solution.py:59
  53.9 2.7 %fusion.407 = f32[16,768]{1,0:T(8,128)S(1)} fusion(bf16[2408,16]{0,1:T(8,128)(2,1)S(1)} %concatenate.56, bf16[2408,768]{1,0:T(8,128)(2,1)} %param.13), kind=kOutput, calls=%fused_computation.483 | convolution fusion | flops 59179008 | bytes 3824896 | tf_op jit(solution)/shard_map/dot_general | solution.py:61
  56.6 2.3 collective-permute-start.6
  58.8 1.3 collective-permute-start.5
  60.3 10.8 %gather_fusion = f32[3072,16]{1,0:T(8,128)} fusion(f32[16,768]{0,1:T(8,128)S(1)} %copy.24, s32[3072]{0:T(1024)S(1)} %broadcast_clamp_fusion), kind=kCustom, calls=%fused_computation | custom fusion | bytes 405504 | tf_op jit(solution)/shard_map/gather | solution.py:66
  71.2 1.6 reduce.3
  73.0 3.8 %collective-permute-start.8 = (f32[1,768]{1,0:T(1,128)S(1)}, f32[1,768]{1,0:T(1,128)S(1)}, u32[]{:S(2)}, u32[]{:S(2)}) collective-permute-start(f32[1,768]{1,0:T(1,128)S(1)} %get-tuple-element.13), channel_id=1, source_target_pairs={{0,1},{1,2},{2,3},{4,5},{5,6},{6,7},{8,9},{9,10},{10,11},{12,13},{... | collective-permute-start | bytes 9224 | tf_op jit(solution)/shard_map/ppermute | solution.py:19
  76.8 1.3 collective-permute-start.7
  78.1 3.0 %collective-permute-done.7 = f32[1,768]{1,0:T(1,128)S(1)} collective-permute-done((f32[1,768]{1,0:T(1,128)S(1)}, f32[1,768]{1,0:T(1,128)S(1)}, u32[]{:S(2)}, u32[]{:S(2)}) %collective-permute-start.7) | collective-permute-done | bytes 3104 | tf_op jit(solution)/shard_map/ppermute | solution.py:20
  81.1 3.1 %convolution_bitcast_fusion.1 = f32[2408,16]{0,1:T(8,128)S(1)} fusion(bf16[2408,768]{1,0:T(8,128)(2,1)} %param.13, f32[16,768]{1,0:T(8,128)S(1)} %fusion.36, f32[1,768]{1,0:T(1,128)S(1)} %collective-permute-done.8, f32[1,768]{1,0:T(1,128)S(1)} %collective-permute-done.7, f32[16,768]{1,0:T(8,128)S(1)} %copy-done.2, f32[16]{0:T(128)S(1)} %copy-done.6), kind=kOutput, calls=%fused_computation.4 | convolution fusion | flops 59277312 | bytes 3957312 | tf_op jit(solution)/shard_map/dot_general | solution.py:53
  84.2 1.5 collective-permute-start.9
  85.8 4.0 %collective-permute-done.9 = f32[2408,16]{0,1:T(8,128)S(1)} collective-permute-done((f32[2408,16]{0,1:T(8,128)S(1)}, f32[2408,16]{0,1:T(8,128)S(1)}, u32[]{:S(2)}, u32[]{:S(2)}) %collective-permute-start.9) | collective-permute-done | bytes 154144 | tf_op jit(solution)/shard_map/ppermute | solution.py:58
  90.5 6.0 %collective-permute-done.10 = f32[2408,16]{0,1:T(8,128)S(1)} collective-permute-done((f32[2408,16]{0,1:T(8,128)S(1)}, f32[2408,16]{0,1:T(8,128)S(1)}, u32[]{:S(2)}, u32[]{:S(2)}) %collective-permute-start.10) | collective-permute-done | bytes 154144 | tf_op jit(solution)/shard_map/ppermute | solution.py:58
  96.5 1.8 collective-permute-start.11
  98.3 8.5 %collective-permute-done.11 = f32[2408,16]{0,1:T(8,128)S(1)} collective-permute-done((f32[2408,16]{0,1:T(8,128)S(1)}, f32[2408,16]{0,1:T(8,128)S(1)}, u32[]{:S(2)}, u32[]{:S(2)}) %collective-permute-start.11) | collective-permute-done | bytes 154144 | tf_op jit(solution)/shard_map/ppermute | solution.py:58
  106.9 6.8 %all_gather.10 = f32[2408,64]{0,1:T(8,128)S(1)} all-gather(f32[2408,16]{0,1:T(8,128)S(1)} %add.85), channel_id=1, replica_groups=mesh['lat'=8,'rad'=4] {'rad'}, dimensions={1}, use_global_device_ids=true | all-gather | bytes 770560 | tf_op jit(solution)/shard_map/all_gather | solution.py:59
  125.7 2.6 %fusion.408 = f32[16,768]{1,0:T(8,128)S(1)} fusion(bf16[2408,16]{0,1:T(8,128)(2,1)S(1)} %concatenate.61, bf16[2408,768]{1,0:T(8,128)(2,1)} %param.13), kind=kOutput, calls=%fused_computation.484 | convolution fusion | flops 59179008 | bytes 3824896 | tf_op jit(solution)/shard_map/dot_general | solution.py:61
  128.4 2.3 collective-permute-start.13
  130.7 1.3 collective-permute-start.12
  132.1 10.8 %gather_fusion.1 = f32[3072,16]{1,0:T(8,128)} fusion(f32[16,768]{0,1:T(8,128)S(1)} %copy.34, s32[3072]{0:T(1024)S(1)} %broadcast_clamp_fusion), kind=kCustom, calls=%fused_computation.1 | custom fusion | bytes 405504 | tf_op jit(solution)/shard_map/gather | solution.py:66
  143.0 1.6 reduce.4
  144.7 3.8 %collective-permute-start.15 = (f32[1,768]{1,0:T(1,128)S(1)}, f32[1,768]{1,0:T(1,128)S(1)}, u32[]{:S(2)}, u32[]{:S(2)}) collective-permute-start(f32[1,768]{1,0:T(1,128)S(1)} %get-tuple-element.9), channel_id=1, source_target_pairs={{0,1},{1,2},{2,3},{4,5},{5,6},{6,7},{8,9},{9,10},{10,11},{12,13},{... | collective-permute-start | bytes 9224 | tf_op jit(solution)/shard_map/ppermute | solution.py:19
  148.5 1.3 collective-permute-start.14
  149.8 3.0 %collective-permute-done.14 = f32[1,768]{1,0:T(1,128)S(1)} collective-permute-done((f32[1,768]{1,0:T(1,128)S(1)}, f32[1,768]{1,0:T(1,128)S(1)}, u32[]{:S(2)}, u32[]{:S(2)}) %collective-permute-start.14) | collective-permute-done | bytes 3104 | tf_op jit(solution)/shard_map/ppermute | solution.py:20
  152.8 3.1 %convolution_bitcast_fusion = f32[2408,16]{0,1:T(8,128)S(1)} fusion(bf16[2408,768]{1,0:T(8,128)(2,1)} %param.13, f32[16,768]{1,0:T(8,128)S(1)} %fusion.24, f32[1,768]{1,0:T(1,128)S(1)} %collective-permute-done.15, f32[1,768]{1,0:T(1,128)S(1)} %collective-permute-done.14, f32[16,768]{1,0:T(8,128)S(1)} %copy-done.2, f32[16]{0:T(128)S(1)} %copy-done.6), kind=kOutput, calls=%fused_computation.3 | convolution fusion | flops 59277312 | bytes 3957312 | tf_op jit(solution)/shard_map/dot_general | solution.py:53
  155.9 1.5 collective-permute-start.16
  157.5 4.0 %collective-permute-done.16 = f32[2408,16]{0,1:T(8,128)S(1)} collective-permute-done((f32[2408,16]{0,1:T(8,128)S(1)}, f32[2408,16]{0,1:T(8,128)S(1)}, u32[]{:S(2)}, u32[]{:S(2)}) %collective-permute-start.16) | collective-permute-done | bytes 154144 | tf_op jit(solution)/shard_map/ppermute | solution.py:58
  161.6 6.6 %collective-permute-done.17 = f32[2408,16]{0,1:T(8,128)S(1)} collective-permute-done((f32[2408,16]{0,1:T(8,128)S(1)}, f32[2408,16]{0,1:T(8,128)S(1)}, u32[]{:S(2)}, u32[]{:S(2)}) %collective-permute-start.17) | collective-permute-done | bytes 154144 | tf_op jit(solution)/shard_map/ppermute | solution.py:58
  169.4 9.1 %collective-permute-done.18 = f32[2408,16]{0,1:T(8,128)S(1)} collective-permute-done((f32[2408,16]{0,1:T(8,128)S(1)}, f32[2408,16]{0,1:T(8,128)S(1)}, u32[]{:S(2)}, u32[]{:S(2)}) %collective-permute-start.18) | collective-permute-done | bytes 154144 | tf_op jit(solution)/shard_map/ppermute | solution.py:58
  178.6 7.4 %all_gather.11 = f32[2408,64]{0,1:T(8,128)S(1)} all-gather(f32[2408,16]{0,1:T(8,128)S(1)} %add.92), channel_id=1, replica_groups=mesh['lat'=8,'rad'=4] {'rad'}, dimensions={1}, use_global_device_ids=true | all-gather | bytes 770560 | tf_op jit(solution)/shard_map/all_gather | solution.py:59
  198.1 2.6 %fusion.409 = f32[16,768]{1,0:T(8,128)S(1)} fusion(bf16[2408,16]{0,1:T(8,128)(2,1)S(1)} %concatenate.66, bf16[2408,768]{1,0:T(8,128)(2,1)} %param.13), kind=kOutput, calls=%fused_computation.485 | convolution fusion | flops 59179008 | bytes 3824896 | tf_op jit(solution)/shard_map/dot_general | solution.py:61
  200.8 2.3 collective-permute-start.20
  203.0 1.3 collective-permute-start.19
  204.5 10.8 %gather_fusion.2 = f32[3072,16]{1,0:T(8,128)} fusion(f32[16,768]{0,1:T(8,128)S(1)} %copy.44, s32[3072]{0:T(1024)S(1)} %broadcast_clamp_fusion), kind=kCustom, calls=%fused_computation.2 | custom fusion | bytes 405504 | tf_op jit(solution)/shard_map/gather | solution.py:66
  215.3 1.6 reduce.5
  217.0 1.4 multiply_reduce_fusion.2
  218.4 2.0 pad_maximum_fusion.12
  220.4 40.0 %psum.7 = f32[3]{0:T(128)S(1)} all-reduce(f32[3]{0:T(128)S(1)} %pad_maximum_fusion.12), channel_id=1, replica_groups=mesh['lat'=8,'rad'=4] {'lat','rad'}, use_global_device_ids=true, to_apply=%region_6.0 | all-reduce | flops 3 | bytes 24 | tf_op jit(solution)/shard_map/psum | solution.py:72
  (231 shorter events, 40.9 us)
Async XLA Ops:
  0.6 41.3 %copy-start = (f32[49,64,64]{2,1,0:T(8,128)S(1)}, f32[49,64,64]{2,1,0:T(8,128)}, u32[]{:S(2)}) copy-start(f32[49,64,64]{2,1,0:T(8,128)} %param.15) | copy-start | bytes 2408452
  1.5 3.7 %collective-permute-start.1 = (f32[1,768]{1,0:T(1,128)S(1)}, f32[1,768]{1,0:T(1,128)S(1)}, u32[]{:S(2)}, u32[]{:S(2)}) collective-permute-start(f32[1,768]{1,0:T(1,128)S(1)} %get-tuple-element.17), channel_id=1, source_target_pairs={{0,1},{1,2},{2,3},{4,5},{5,6},{6,7},{8,9},{9,10},{10,11},{12,13},{... | collective-permute-start | bytes 9224 | tf_op jit(solution)/shard_map/ppermute | solution.py:19
  3.9 23.4 %copy-start.5 = (s32[4,768]{1,0:T(4,128)S(1)}, s32[4,768]{1,0:T(4,128)}, u32[]{:S(2)}) copy-start(s32[4,768]{1,0:T(4,128)} %param.14) | copy-start | bytes 36868
  3.9 5.2 %collective-permute-start = (f32[1,768]{1,0:T(1,128)S(1)}, f32[1,768]{1,0:T(1,128)S(1)}, u32[]{:S(2)}, u32[]{:S(2)}) collective-permute-start(f32[1,768]{1,0:T(1,128)S(1)} %get-tuple-element.16), channel_id=1, source_target_pairs={{1,0},{2,1},{3,2},{5,4},{6,5},{7,6},{9,8},{10,9},{11,10},{13,12},{... | collective-permute-start | bytes 9224 | tf_op jit(solution)/shard_map/ppermute | solution.py:20
  12.3 5.5 %collective-permute-start.2 = (f32[2408,16]{0,1:T(8,128)S(1)}, f32[2408,16]{0,1:T(8,128)S(1)}, u32[]{:S(2)}, u32[]{:S(2)}) collective-permute-start(f32[2408,16]{0,1:T(8,128)S(1)} %convolution_bitcast_fusion.2), channel_id=1, source_target_pairs={{0,4},{4,0},{8,12},{12,8},{16,20},{20,16},{24,28},{28,24},{1,5},{5... | collective-permute-start | bytes 462344 | tf_op jit(solution)/shard_map/ppermute | solution.py:58
  17.9 6.7 %collective-permute-start.3 = (f32[2408,16]{0,1:T(8,128)S(1)}, f32[2408,16]{0,1:T(8,128)S(1)}, u32[]{:S(2)}, u32[]{:S(2)}) collective-permute-start(f32[2408,16]{0,1:T(8,128)S(1)} %add.74), channel_id=1, source_target_pairs={{0,8},{4,12},{8,0},{12,4},{16,24},{20,28},{24,16},{28,20},{1,9},{5... | collective-permute-start | bytes 462344 | tf_op jit(solution)/shard_map/ppermute | solution.py:58
  24.6 10.3 %collective-permute-start.4 = (f32[2408,16]{0,1:T(8,128)S(1)}, f32[2408,16]{0,1:T(8,128)S(1)}, u32[]{:S(2)}, u32[]{:S(2)}) collective-permute-start(f32[2408,16]{0,1:T(8,128)S(1)} %add.75), channel_id=1, source_target_pairs={{0,16},{4,20},{8,24},{12,28},{16,0},{20,4},{24,8},{28,12},{1,17},{... | collective-permute-start | bytes 462344 | tf_op jit(solution)/shard_map/ppermute | solution.py:58
  53.9 6.3 %copy-start.1 = (f32[16,768]{1,0:T(8,128)S(1)}, f32[16,768]{1,0:T(8,128)}, u32[]{:S(2)}) copy-start(f32[16,768]{1,0:T(8,128)} %param.8) | copy-start | bytes 147460
  56.6 16.3 %collective-permute-start.6 = (f32[1,768]{1,0:T(1,128)S(1)}, f32[1,768]{1,0:T(1,128)S(1)}, u32[]{:S(2)}, u32[]{:S(2)}) collective-permute-start(f32[1,768]{1,0:T(1,128)S(1)} %get-tuple-element.15), channel_id=1, source_target_pairs={{0,1},{1,2},{2,3},{4,5},{5,6},{6,7},{8,9},{9,10},{10,11},{12,13},{... | collective-permute-start | bytes 9224 | tf_op jit(solution)/shard_map/ppermute | solution.py:19
  58.8 14.1 %collective-permute-start.5 = (f32[1,768]{1,0:T(1,128)S(1)}, f32[1,768]{1,0:T(1,128)S(1)}, u32[]{:S(2)}, u32[]{:S(2)}) collective-permute-start(f32[1,768]{1,0:T(1,128)S(1)} %get-tuple-element.14), channel_id=1, source_target_pairs={{1,0},{2,1},{3,2},{5,4},{6,5},{7,6},{9,8},{10,9},{11,10},{13,12},{... | collective-permute-start | bytes 9224 | tf_op jit(solution)/shard_map/ppermute | solution.py:20
  71.2 1.8 copy-start.3
  71.2 1.8 copy-start.4
  71.2 9.9 %copy-start.2 = (f32[16,768]{1,0:T(8,128)S(1)}, f32[16,768]{1,0:T(8,128)}, u32[]{:S(2)}) copy-start(f32[16,768]{1,0:T(8,128)} %param.10) | copy-start | bytes 147460
  71.2 9.9 %copy-start.6 = (f32[16]{0:T(128)S(1)}, f32[16]{0:T(128)}, u32[]{:S(2)}) copy-start(f32[16]{0:T(128)} %param.11) | copy-start | bytes 196
  73.0 5.1 %collective-permute-start.8 = (f32[1,768]{1,0:T(1,128)S(1)}, f32[1,768]{1,0:T(1,128)S(1)}, u32[]{:S(2)}, u32[]{:S(2)}) collective-permute-start(f32[1,768]{1,0:T(1,128)S(1)} %get-tuple-element.13), channel_id=1, source_target_pairs={{0,1},{1,2},{2,3},{4,5},{5,6},{6,7},{8,9},{9,10},{10,11},{12,13},{... | collective-permute-start | bytes 9224 | tf_op jit(solution)/shard_map/ppermute | solution.py:19
  76.8 4.3 %collective-permute-start.7 = (f32[1,768]{1,0:T(1,128)S(1)}, f32[1,768]{1,0:T(1,128)S(1)}, u32[]{:S(2)}, u32[]{:S(2)}) collective-permute-start(f32[1,768]{1,0:T(1,128)S(1)} %get-tuple-element.12), channel_id=1, source_target_pairs={{1,0},{2,1},{3,2},{5,4},{6,5},{7,6},{9,8},{10,9},{11,10},{13,12},{... | collective-permute-start | bytes 9224 | tf_op jit(solution)/shard_map/ppermute | solution.py:20
  84.2 5.5 %collective-permute-start.9 = (f32[2408,16]{0,1:T(8,128)S(1)}, f32[2408,16]{0,1:T(8,128)S(1)}, u32[]{:S(2)}, u32[]{:S(2)}) collective-permute-start(f32[2408,16]{0,1:T(8,128)S(1)} %convolution_bitcast_fusion.1), channel_id=1, source_target_pairs={{0,4},{4,0},{8,12},{12,8},{16,20},{20,16},{24,28},{28,24},{1,5},{5... | collective-permute-start | bytes 462344 | tf_op jit(solution)/shard_map/ppermute | solution.py:58
  89.8 6.7 %collective-permute-start.10 = (f32[2408,16]{0,1:T(8,128)S(1)}, f32[2408,16]{0,1:T(8,128)S(1)}, u32[]{:S(2)}, u32[]{:S(2)}) collective-permute-start(f32[2408,16]{0,1:T(8,128)S(1)} %add.83), channel_id=1, source_target_pairs={{0,8},{4,12},{8,0},{12,4},{16,24},{20,28},{24,16},{28,20},{1,9},{5... | collective-permute-start | bytes 462344 | tf_op jit(solution)/shard_map/ppermute | solution.py:58
  96.5 10.3 %collective-permute-start.11 = (f32[2408,16]{0,1:T(8,128)S(1)}, f32[2408,16]{0,1:T(8,128)S(1)}, u32[]{:S(2)}, u32[]{:S(2)}) collective-permute-start(f32[2408,16]{0,1:T(8,128)S(1)} %add.84), channel_id=1, source_target_pairs={{0,16},{4,20},{8,24},{12,28},{16,0},{20,4},{24,8},{28,12},{1,17},{... | collective-permute-start | bytes 462344 | tf_op jit(solution)/shard_map/ppermute | solution.py:58
  128.4 16.3 %collective-permute-start.13 = (f32[1,768]{1,0:T(1,128)S(1)}, f32[1,768]{1,0:T(1,128)S(1)}, u32[]{:S(2)}, u32[]{:S(2)}) collective-permute-start(f32[1,768]{1,0:T(1,128)S(1)} %get-tuple-element.11), channel_id=1, source_target_pairs={{0,1},{1,2},{2,3},{4,5},{5,6},{6,7},{8,9},{9,10},{10,11},{12,13},{... | collective-permute-start | bytes 9224 | tf_op jit(solution)/shard_map/ppermute | solution.py:19
  130.7 14.0 %collective-permute-start.12 = (f32[1,768]{1,0:T(1,128)S(1)}, f32[1,768]{1,0:T(1,128)S(1)}, u32[]{:S(2)}, u32[]{:S(2)}) collective-permute-start(f32[1,768]{1,0:T(1,128)S(1)} %get-tuple-element.10), channel_id=1, source_target_pairs={{1,0},{2,1},{3,2},{5,4},{6,5},{7,6},{9,8},{10,9},{11,10},{13,12},{... | collective-permute-start | bytes 9224 | tf_op jit(solution)/shard_map/ppermute | solution.py:20
  144.7 5.1 %collective-permute-start.15 = (f32[1,768]{1,0:T(1,128)S(1)}, f32[1,768]{1,0:T(1,128)S(1)}, u32[]{:S(2)}, u32[]{:S(2)}) collective-permute-start(f32[1,768]{1,0:T(1,128)S(1)} %get-tuple-element.9), channel_id=1, source_target_pairs={{0,1},{1,2},{2,3},{4,5},{5,6},{6,7},{8,9},{9,10},{10,11},{12,13},{... | collective-permute-start | bytes 9224 | tf_op jit(solution)/shard_map/ppermute | solution.py:19
  148.5 4.3 %collective-permute-start.14 = (f32[1,768]{1,0:T(1,128)S(1)}, f32[1,768]{1,0:T(1,128)S(1)}, u32[]{:S(2)}, u32[]{:S(2)}) collective-permute-start(f32[1,768]{1,0:T(1,128)S(1)} %get-tuple-element.8), channel_id=1, source_target_pairs={{1,0},{2,1},{3,2},{5,4},{6,5},{7,6},{9,8},{10,9},{11,10},{13,12},{... | collective-permute-start | bytes 9224 | tf_op jit(solution)/shard_map/ppermute | solution.py:20
  155.9 5.5 %collective-permute-start.16 = (f32[2408,16]{0,1:T(8,128)S(1)}, f32[2408,16]{0,1:T(8,128)S(1)}, u32[]{:S(2)}, u32[]{:S(2)}) collective-permute-start(f32[2408,16]{0,1:T(8,128)S(1)} %convolution_bitcast_fusion), channel_id=1, source_target_pairs={{0,4},{4,0},{8,12},{12,8},{16,20},{20,16},{24,28},{28,24},{1,5},{5... | collective-permute-start | bytes 462344 | tf_op jit(solution)/shard_map/ppermute | solution.py:58
  161.5 6.7 %collective-permute-start.17 = (f32[2408,16]{0,1:T(8,128)S(1)}, f32[2408,16]{0,1:T(8,128)S(1)}, u32[]{:S(2)}, u32[]{:S(2)}) collective-permute-start(f32[2408,16]{0,1:T(8,128)S(1)} %add.90), channel_id=1, source_target_pairs={{0,8},{4,12},{8,0},{12,4},{16,24},{20,28},{24,16},{28,20},{1,9},{5... | collective-permute-start | bytes 462344 | tf_op jit(solution)/shard_map/ppermute | solution.py:58
  168.2 10.3 %collective-permute-start.18 = (f32[2408,16]{0,1:T(8,128)S(1)}, f32[2408,16]{0,1:T(8,128)S(1)}, u32[]{:S(2)}, u32[]{:S(2)}) collective-permute-start(f32[2408,16]{0,1:T(8,128)S(1)} %add.91), channel_id=1, source_target_pairs={{0,16},{4,20},{8,24},{12,28},{16,0},{20,4},{24,8},{28,12},{1,17},{... | collective-permute-start | bytes 462344 | tf_op jit(solution)/shard_map/ppermute | solution.py:58
  200.8 16.3 %collective-permute-start.20 = (f32[1,768]{1,0:T(1,128)S(1)}, f32[1,768]{1,0:T(1,128)S(1)}, u32[]{:S(2)}, u32[]{:S(2)}) collective-permute-start(f32[1,768]{1,0:T(1,128)S(1)} %get-tuple-element.7), channel_id=1, source_target_pairs={{0,1},{1,2},{2,3},{4,5},{5,6},{6,7},{8,9},{9,10},{10,11},{12,13},{... | collective-permute-start | bytes 9224 | tf_op jit(solution)/shard_map/ppermute | solution.py:19
  203.0 14.0 %collective-permute-start.19 = (f32[1,768]{1,0:T(1,128)S(1)}, f32[1,768]{1,0:T(1,128)S(1)}, u32[]{:S(2)}, u32[]{:S(2)}) collective-permute-start(f32[1,768]{1,0:T(1,128)S(1)} %get-tuple-element.6), channel_id=1, source_target_pairs={{1,0},{2,1},{3,2},{5,4},{6,5},{7,6},{9,8},{10,9},{11,10},{13,12},{... | collective-permute-start | bytes 9224 | tf_op jit(solution)/shard_map/ppermute | solution.py:20
